TPU v7x, 32 devices: a whole 2x2x4 slice. The times are simulated.
32 devices in a mesh: band: 2 (over x), domain: 16 (over z, y, core).
Axes of the slice: x: 2, y: 2, z: 4, core: 2. Of those that a mesh axis runs over, the one named last changes fastest.
Arguments:
- dens_part: float32 [2, 171, 36864], P('band', None, 'domain'), may hold values from -3 to 3
- counts: int32 [16], P('domain'), may hold values from 1 to 2304, 12288 in all
- gaunt: float32 [171, 525], replicated, may hold values from -0.4375 to 0.4375
- pair_waves: float32 [21, 400], replicated, may hold values from -1.25 to 1.25
- y_table: float32 [25, 50], replicated, may hold values from -1.25 to 1.25
- core: float32 [400], replicated, may hold values from 1 to 4
- radial_weights: float32 [400], replicated, may hold values from 0.0001 to 0.001
Outputs:
- dh_packed: float32 [171, 36864], P(None, 'domain')
- atom_energy: float32 [36864], P('domain')
Inputs may be any that keep to these rules, and one draw needn't show every extreme that they name: `counts`: atoms owned by each domain; they sum to 12288, and some domain owns exactly 2304.
All inputs are finite; a program needn't handle non-finite values. No bound on the sum of `counts` on one device may be relied on, other than what follows from the above.
Results may differ from a plain program's by a relative error of at most 0.0003.
Values sent between devices are 32-bit elements; how exact they have to be, the bound alone decides.
A program may use at most 128 MiB of HBM per device.

v0:
```python
import jax
import jax.numpy as jnp
from jax import lax
from jax.sharding import PartitionSpec as P

highest = lax.Precision.HIGHEST


def local_energy(density_rows, gaunt, pair_waves, y_table, core, radial_weights):
    atom_count = density_rows.shape[0]
    harmonics = y_table.shape[0]
    pair_count = pair_waves.shape[0]
    directions = y_table.shape[1]
    coefficients = jnp.dot(
        density_rows, gaunt, precision=highest, preferred_element_type=jnp.float32
    )
    coefficients = coefficients.reshape(atom_count * harmonics, pair_count)
    radial = jnp.dot(
        coefficients, pair_waves, precision=highest, preferred_element_type=jnp.float32
    )
    radial = radial.reshape(atom_count, harmonics, pair_waves.shape[1])
    points = jnp.einsum("ln,alg->ang", y_table, radial, precision=highest) + core[None, None, :]
    smooth = jnp.sqrt(points * points + 0.25)
    cube_root = jnp.cbrt(smooth)
    wigner_radius = 0.6203504908994 / cube_root
    denominator = 7.8 + wigner_radius
    energy_density = -0.7385587663820224 * smooth * cube_root - 0.44 * smooth / denominator
    slope = -0.9847450218426965 * cube_root - 0.44 * (
        1.0 / denominator + wigner_radius / (3.0 * denominator * denominator)
    )
    point_weight = 4.0 * jnp.pi / directions * radial_weights
    energy = jnp.sum(energy_density * point_weight[None, None, :], axis=(1, 2))
    potential = point_weight[None, None, :] * slope * points / smooth
    back_radial = jnp.einsum("ln,ang->alg", y_table, potential, precision=highest)
    back_coef = jnp.dot(
        back_radial.reshape(atom_count * harmonics, pair_waves.shape[1]),
        pair_waves.T,
        precision=highest,
        preferred_element_type=jnp.float32,
    )
    back_coef = back_coef.reshape(atom_count, harmonics * pair_count)
    hamiltonian = jnp.dot(back_coef, gaunt.T, precision=highest, preferred_element_type=jnp.float32)
    return (hamiltonian, energy)


def per_device(dens_part, counts, gaunt, pair_waves, y_table, core, radial_weights):
    band_count = lax.axis_size("band")
    domain_count = lax.axis_size("domain")
    band_index = lax.axis_index("band")
    domain_index = lax.axis_index("domain")
    entries = dens_part.shape[1]
    slot_total = dens_part.shape[2]
    share = slot_total // band_count
    grouped = dens_part.reshape(entries, share, band_count)
    own_cols = lax.psum_scatter(grouped, "band", scatter_dimension=2, tiled=True)[:, :, 0]
    own_rows = own_cols.T
    slot_ids = jnp.arange(share, dtype=jnp.int32) * band_count + band_index
    is_alive = slot_ids < counts[0]
    own_rows = jnp.where(is_alive[:, None], own_rows, jnp.zeros_like(own_rows))
    every_count = lax.all_gather(counts, "domain", axis=0, tiled=True)
    live_rows = jnp.maximum((every_count - band_index + band_count - 1) // band_count, 0)
    starts = jnp.cumsum(live_rows) - live_rows
    domain_ids = jnp.arange(domain_count, dtype=jnp.int32)
    own_start = jnp.sum(jnp.where(domain_ids == domain_index, starts, 0))
    own_live = jnp.sum(jnp.where(domain_ids == domain_index, live_rows, 0))
    capacity = (share + domain_count - 1) // domain_count
    worker_rows = slot_total // 3 // band_count + 1
    position_ids = jnp.arange(capacity, dtype=jnp.int32)
    send_offset = (domain_ids - own_start) % domain_count
    send_row = send_offset[:, None] + position_ids[None, :] * domain_count
    send_valid = send_row < own_live
    picked = jnp.take(own_rows, jnp.minimum(send_row, share - 1), axis=0)
    outgoing = jnp.where(send_valid[:, :, None], picked, jnp.zeros_like(picked))
    incoming = lax.all_to_all(outgoing, "domain", split_axis=0, concat_axis=0, tiled=True)
    recv_offset = (domain_index - starts) % domain_count
    recv_row = recv_offset[:, None] + position_ids[None, :] * domain_count
    recv_valid = (recv_row < live_rows[:, None]).reshape(-1)
    target_slot = ((starts[:, None] + recv_row - domain_index) // domain_count).reshape(-1)
    worker_ids = jnp.arange(worker_rows, dtype=jnp.int32)
    placement = jnp.where(
        (worker_ids[:, None] == target_slot[None, :]) & recv_valid[None, :], 1.0, 0.0
    ).astype(jnp.float32)
    compact = jnp.dot(
        placement,
        incoming.reshape(domain_count * capacity, entries),
        precision=highest,
        preferred_element_type=jnp.float32,
    )
    work_ham, work_energy = local_energy(compact, gaunt, pair_waves, y_table, core, radial_weights)
    back_ham = jnp.dot(placement.T, work_ham, precision=highest, preferred_element_type=jnp.float32)
    back_energy = jnp.dot(
        placement.T, work_energy[:, None], precision=highest, preferred_element_type=jnp.float32
    )
    returned_ham, returned_energy = (
        lax.all_to_all(
            back_ham.reshape(domain_count, capacity, entries),
            "domain",
            split_axis=0,
            concat_axis=0,
            tiled=True,
        ),
        lax.all_to_all(
            back_energy.reshape(domain_count, capacity),
            "domain",
            split_axis=0,
            concat_axis=0,
            tiled=True,
        ),
    )
    local_ids = jnp.arange(share, dtype=jnp.int32)
    worker_of = (own_start + local_ids) % domain_count
    offset_of = jnp.sum(
        jnp.where(worker_of[:, None] == domain_ids[None, :], send_offset[None, :], 0), axis=1
    )
    flat_index = worker_of * capacity + jnp.minimum(
        (local_ids - offset_of) // domain_count, capacity - 1
    )
    hamiltonian = jnp.take(
        returned_ham.reshape(domain_count * capacity, entries), flat_index, axis=0
    )
    energy = jnp.take(returned_energy.reshape(domain_count * capacity), flat_index, axis=0)
    hamiltonian = jnp.where(is_alive[:, None], hamiltonian, jnp.zeros_like(hamiltonian))
    energy = jnp.where(is_alive, energy, jnp.zeros_like(energy))
    all_ham, all_energy = (
        lax.all_gather(hamiltonian.T[:, :, None], "band", axis=2, tiled=True),
        lax.all_gather(energy[:, None], "band", axis=1, tiled=True),
    )
    return (all_ham.reshape(entries, slot_total), all_energy.reshape(slot_total))


def solution(mesh):
    return jax.shard_map(
        per_device,
        mesh=mesh,
        in_specs=(P("band", None, "domain"), P("domain"), P(), P(), P(), P(), P()),
        out_specs=(P(None, "domain"), P("domain")),
        check_vma=False,
    )
```

profile of v0, /device:TPU:0, one launch (start us, length us, event | category | flops | bytes accessed | tf_op | source)
XLA Modules:
  0.0 533.4 jit_solution(11146826885590146231)
XLA Ops:
  7.2 5.2 copy.32
  12.4 3.0 reshape.441
  15.4 1.6 copy.33
  19.1 13.8 %all-reduce = s32[16]{0:T(128)S(1)} all-reduce(s32[16]{0:T(128)S(1)} %dynamic-update-slice), channel_id=1, replica_groups=mesh['band'=2,'domain'=16] {'domain'}, use_global_device_ids=true, to_apply=%add | all-reduce | flops 16 | bytes 128
  35.9 18.9 %reduce-scatter.2.cloned.1.call-done = f32[171,1152,1]{0,1,2:T(8,128)} async-done(((f32[171,1152,2]{0,1,2:T(8,128)}), f32[171,1152,1]{0,1,2:T(8,128)}) %reduce-scatter.2.cloned.1.call-update) | async-done | bytes 787984 | tf_op jit(solution)/shard_map/reduce_scatter | solution.py:55
  54.7 1.5 fusion.42
  56.3 3.3 gather_fusion
  59.5 1.3 select_select_fusion
  60.8 5.8 %all-to-all-start = ((f32[16,72,171]{2,1,0:T(8,128)}), f32[16,72,171]{2,1,0:T(8,128)S(1)}, u32[]{:S(2)}, u32[]{:S(2)}) async-start(f32[16,72,171]{2,1,0:T(8,128)} %select_select_fusion), calls=%async_computation.1 | async-start | bytes 2359296 | tf_op jit(solution)/shard_map/all_to_all | solution.py:74
  67.5 24.1 %all-to-all-done = f32[16,72,171]{2,1,0:T(8,128)S(1)} async-done(((f32[16,72,171]{2,1,0:T(8,128)}), f32[16,72,171]{2,1,0:T(8,128)S(1)}, u32[]{:S(2)}, u32[]{:S(2)}) %all-to-all-start) | async-done | bytes 788000 | tf_op jit(solution)/shard_map/all_to_all | solution.py:74
  91.6 2.7 fusion.33
  94.4 1.3 fusion.102
  95.9 16.9 %fusion.58 = f32[385,25,400]{2,0,1:T(8,128)S(1)} fusion(f32[385,25,21]{0,2,1:T(8,128)S(1)} %dot_general.31, f32[21,400]{1,0:T(8,128)S(1)} %copy-done.1), kind=kOutput, calls=%fused_computation.63 | convolution fusion | flops 970199936 | bytes 16242100 | tf_op jit(solution)/shard_map/dot_general | solution.py:18
  112.8 165.9 %multiply_reduce_fusion = (f32[385]{0:T(512)}, f32[385,400,50]{1,2,0:T(8,128)}) fusion(f32[400]{0:T(512)S(1)} %copy-done.16, f32[400]{0:T(512)S(1)} %broadcast_multiply_fusion, f32[25,50]{1,0:T(8,128)S(1)} %copy-done.15, f32[385,25,400]{2,0,1:T(8,128)S(1)} %fusion.58), kind=kOutput, calls=%fused_computation.15 | convolution fusion | flops 2402399744 | bytes 46209740 | tf_op jit(solution)/shard_map/ln,alg->ang/dot_general | solution.py:22
  278.7 119.0 %fusion.28 = f32[385,25,400]{2,1,0:T(8,128)} fusion(f32[385,400,50]{1,2,0:T(8,128)} %get-tuple-element.18, f32[400]{0:T(512)S(1)} %copy-done.16, f32[400]{0:T(512)S(1)} %broadcast_multiply_fusion, f32[25,50]{1,0:T(8,128)S(1)} %copy-done.15), kind=kOutput, calls=%fused_computation.33 | convolution fusion | flops 2440900096 | bytes 46208200 | tf_op jit(solution)/shard_map/ln,ang->alg/dot_general | solution.py:34
  397.7 21.1 %reshape.443 = f32[9625,400]{1,0:T(8,128)} reshape(f32[385,25,400]{2,1,0:T(8,128)} %fusion.28) | data formatting | bytes 30800000 | tf_op jit(solution)/shard_map/reshape | solution.py:36
  418.7 19.7 %fusion.103 = f32[9625,21]{1,0:T(8,128)} fusion(f32[9625,400]{1,0:T(8,128)} %reshape.443, f32[21,400]{1,0:T(8,128)S(1)} %copy-done.2), kind=kOutput, calls=%fused_computation.162 | convolution fusion | flops 970199936 | bytes 16242100 | tf_op jit(solution)/shard_map/dot_general | solution.py:35
  438.4 3.8 reshape.444
  442.2 1.2 fusion.104
  443.5 4.1 fusion.31
  447.5 7.4 %all-to-all-start.1 = ((f32[16,72,171]{2,1,0:T(8,128)}), f32[16,72,171]{2,1,0:T(8,128)S(1)}, u32[]{:S(2)}, u32[]{:S(2)}) async-start(f32[16,72,171]{2,1,0:T(8,128)} %bitcast.11), calls=%async_computation.2 | async-start | bytes 2359296 | tf_op jit(solution)/shard_map/all_to_all | solution.py:95
  456.9 23.1 %all-to-all-done.1 = f32[16,72,171]{2,1,0:T(8,128)S(1)} async-done(((f32[16,72,171]{2,1,0:T(8,128)}), f32[16,72,171]{2,1,0:T(8,128)S(1)}, u32[]{:S(2)}, u32[]{:S(2)}) %all-to-all-start.1) | async-done | bytes 788000 | tf_op jit(solution)/shard_map/all_to_all | solution.py:95
  480.0 3.5 gather_fusion.1
  484.5 1.2 copy.38
  485.8 3.4 fusion.47
  489.2 13.7 %all_to_all.19 = f32[16,1,72]{2,1,0:T(1,128)S(1)} all-to-all(f32[16,1,72]{2,1,0:T(1,128)S(1)} %fusion.47), channel_id=1, replica_groups=mesh['band'=2,'domain'=16] {'domain'}, dimensions={0} | all-to-all | bytes 9216 | tf_op jit(solution)/shard_map/all_to_all | solution.py:102
  504.1 6.5 %gather_fusion.2 = f32[1152]{0:T(1024)S(1)} fusion(f32[1152]{0:T(1024)S(1)} %reshape.448, s32[2048]{0:T(1024)S(1)} %pad_clamp_fusion), kind=kCustom, calls=%fused_computation.2 | custom fusion | bytes 13824 | tf_op jit(solution)/shard_map/jit(_take)/gather | solution.py:121
  511.2 4.4 all-gather
  515.9 0.9 reshape.449
  516.8 3.8 copy.39
  520.6 2.7 reshape.447
  523.3 2.9 copy.41
  (77 shorter events, 10.4 us)
Async XLA Ops:
  7.2 87.2 %copy-start = (f32[171,525]{1,0:T(8,128)S(1)}, f32[171,525]{1,0:T(8,128)}, u32[]{:S(2)}) copy-start(f32[171,525]{1,0:T(8,128)} %param.9) | copy-start | bytes 1077304
  7.2 47.6 %reduce-scatter.2.cloned.1.call-start = ((), (), s32[]{:S(2)}) async-start(), calls=%async_computation.4 | async-start | bytes 3538944 | tf_op jit(solution)/shard_map/reduce_scatter | solution.py:55
  12.4 5.3 copy-start.17
  34.9 0.9 copy-start.10
  35.1 19.7 %copy-start.3 = (pred[1152]{0:T(1024)(128)(4,1)}, pred[1152]{0:T(1024)(128)(4,1)S(1)}, u32[]{:S(2)}) copy-start(pred[1152]{0:T(1024)(128)(4,1)S(1)} %add_compare_fusion.2) | copy-start | bytes 3460
  35.8 30.7 %copy-start.5 = (pred[16,72]{1,0:T(8,128)(4,1)}, pred[16,72]{1,0:T(8,128)(4,1)S(1)}, u32[]{:S(2)}) copy-start(pred[16,72]{1,0:T(8,128)(4,1)S(1)} %get-tuple-element.16) | copy-start | bytes 3460
  56.2 11.2 %copy-start.12 = (f32[400]{0:T(512)S(1)}, f32[400]{0:T(512)}, u32[]{:S(2)}) copy-start(f32[400]{0:T(512)} %param.13) | copy-start | bytes 4804
  60.8 35.0 %copy-start.1 = (f32[21,400]{1,0:T(8,128)S(1)}, f32[21,400]{1,0:T(8,128)}, u32[]{:S(2)}) copy-start(f32[21,400]{1,0:T(8,128)} %param.10) | copy-start | bytes 100804
  60.8 30.8 %all-to-all-start = ((f32[16,72,171]{2,1,0:T(8,128)}), f32[16,72,171]{2,1,0:T(8,128)S(1)}, u32[]{:S(2)}, u32[]{:S(2)}) async-start(f32[16,72,171]{2,1,0:T(8,128)} %select_select_fusion), calls=%async_computation.1 | async-start | bytes 2359296 | tf_op jit(solution)/shard_map/all_to_all | solution.py:74
  66.7 46.1 %copy-start.13 = (pred[1152]{0:T(1024)(128)(4,1)}, pred[1152]{0:T(1024)(128)(4,1)S(1)}, u32[]{:S(2)}) copy-start(pred[1152]{0:T(1024)(128)(4,1)S(1)} %lt.114) | copy-start | bytes 3460
  67.5 26.9 %copy-start.8 = (s32[1152]{0:T(1024)}, s32[1152]{0:T(1024)S(1)}, u32[]{:S(2)}) copy-start(s32[1152]{0:T(1024)S(1)} %add_select_fusion.1) | copy-start | bytes 13828
  95.9 16.9 %copy-start.15 = (f32[25,50]{1,0:T(8,128)S(1)}, f32[25,50]{1,0:T(8,128)}, u32[]{:S(2)}) copy-start(f32[25,50]{1,0:T(8,128)} %param.11) | copy-start | bytes 15004
  95.9 16.9 %copy-start.16 = (f32[400]{0:T(512)S(1)}, f32[400]{0:T(512)}, u32[]{:S(2)}) copy-start(f32[400]{0:T(512)} %param.12) | copy-start | bytes 4804
  397.7 21.1 %copy-start.2 = (f32[21,400]{1,0:T(8,128)S(1)}, f32[21,400]{1,0:T(8,128)}, u32[]{:S(2)}) copy-start(f32[21,400]{1,0:T(8,128)} %param.10) | copy-start | bytes 100804
  438.4 5.0 copy-start.9
  438.4 5.0 copy-start.14
  438.4 17.1 %copy-start.11 = (s32[16]{0:T(128)S(1)}, s32[16]{0:T(128)}, u32[]{:S(2)}) copy-start(s32[16]{0:T(128)} %copy-done.10) | copy-start | bytes 196
  447.5 32.5 %all-to-all-start.1 = ((f32[16,72,171]{2,1,0:T(8,128)}), f32[16,72,171]{2,1,0:T(8,128)S(1)}, u32[]{:S(2)}, u32[]{:S(2)}) async-start(f32[16,72,171]{2,1,0:T(8,128)} %bitcast.11), calls=%async_computation.2 | async-start | bytes 2359296 | tf_op jit(solution)/shard_map/all_to_all | solution.py:95
  455.0 61.8 %all-gather.3.cloned.1.call-start = ((), (), s32[]{:S(2)}) async-start(), calls=%async_computation.5 | async-start | bytes 2433024 | tf_op jit(solution)/shard_map/all_gather | solution.py:125
  480.0 3.5 copy-start.4
  483.5 2.2 copy-start.6
  483.5 2.2 copy-start.7
  483.6 2.2 copy-start.18
Sparse Core Ops, SparseCore 0:
  17.2 37.5 reduce-scatter.1
  485.9 29.6 all-gather.2
where the time goes:
time: 542 us; the launch traced here: 533 us
  matrix products  334 us (62%)
  waiting for transfers between devices  66.2 us (12%)
  local copies, waits for them, and re-layouts  62.2 us (11%)
  blocking collectives  31.8 us (6%)
  between operations  15.6 us (3%)
  starting transfers between devices  13.3 us (2%)
  other arithmetic  10.3 us (2%)
    dot_general x1, matrix products, local_energy(): jnp.einsum('ln,alg->ang', y_table, radial, precision=highest)  166 us
    dot_general x1, matrix products, local_energy(): jnp.einsum('ln,ang->alg', y_table, potential, precision=highest)  119 us
    all_to_all x1, waiting for transfers between devices, per_device(): lax.all_to_all(outgoing, 'domain', split_axis=0, concat_axis=0, tiled=True)  24.1 us
    all_to_all x1, waiting for transfers between devices, per_device(): lax.all_to_all(back_ham.reshape(domain_count, capacity, entries), 'domain...  23.1 us
    reshape x1, local copies, waits for them, and re-layouts, local_energy(): back_radial.reshape(atom_count * harmonics, pair_waves.shape[1])  21.1 us
    dot_general x1, matrix products, local_energy(): jnp.dot(back_radial.reshape(atom_count * harmonics, pair_waves.shape[1]),...  19.7 us
    reduce_scatter x1, waiting for transfers between devices, per_device(): lax.psum_scatter(grouped, 'band', scatter_dimension=2, tiled=True)[:, :, 0]  18.9 us
    dot_general x1, matrix products, local_energy(): jnp.dot(coefficients, pair_waves, precision=highest, preferred_element_ty...  16.9 us
  transfers between devices with their start and end apart: 4, of which 3 were waited for; matrix products, arithmetic and copies ran while one was open for 4% of the time, Pallas kernels for 0%

commit v1 on v0

v1 whole, which is shorter than its diff:
```python
import math

import jax
import jax.numpy as jnp
from jax import lax
from jax.experimental import pallas as pl
from jax.experimental.pallas import tpu as pltpu
from jax.sharding import PartitionSpec as P

highest = lax.Precision.HIGHEST
f32 = jnp.float32
bf16 = jnp.bfloat16

LANES = 128
WIDE = 256

C_RS = 0.6203504908994
EX_A = 0.7385587663820224
EX_D = 0.9847450218426965

def round_up(value, step):
    return -(-value // step) * step

def split(x):
    hi = lax.reduce_precision(x, 8, 7)
    return hi.astype(bf16), (x - hi).astype(bf16)

def atom_kernel(
    dens_ref, gy_ref, gyb_ref, pw_ref, pwb_ref, core_ref, weight_ref,
    ham_ref, energy_ref, pts_ref, hi_ref, lo_ref, eacc_ref, back_ref, *, pairs, step
):
    atoms = dens_ref.shape[1]
    rows = pw_ref.shape[1]
    grid_points = pw_ref.shape[0]
    couples = gy_ref.shape[0]
    chunks = 2 * atoms // WIDE
    eacc_ref[...] = jnp.zeros_like(eacc_ref)

    def mixed(x):
        ids = lax.broadcasted_iota(jnp.int32, x.shape, 0)
        hi = x.astype(bf16).astype(f32)
        low = (ids >= pairs) & (ids < 2 * pairs)
        return jnp.where(low, x - hi, hi).astype(bf16)

    def body(m, carry):
        both = jnp.dot(gy_ref[m], dens_ref[...], preferred_element_type=f32)
        lhs = mixed(jnp.concatenate([both[:rows], both[rows:]], axis=1))
        back = []
        for j in range(chunks):
            cols = lhs[:, j * WIDE:(j + 1) * WIDE]
            pts_ref[j] = jnp.dot(pw_ref[...], cols, preferred_element_type=f32)
            for g in range(0, grid_points, step):
                part = pl.ds(g, step)
                p = pts_ref[j, part, :] + core_ref[part, :]
                u = p * p + 0.25
                v = jnp.exp2(jnp.log(u) * (-1.0 / (6.0 * math.log(2.0))))
                r = v / (7.8 + C_RS * v)
                v2 = v * v
                br = 0.44 * r
                eacc_ref[j, part, :] += (u * v2) * (EX_A + br)
                pot = (p * v2) * (EX_D + (0.44 + (0.44 * C_RS / 3.0) * r) * r)
                hi = pot.astype(bf16)
                hi_ref[j, part, :] = hi
                lo_ref[j, part, :] = (pot - hi.astype(f32)).astype(bf16)
            first = jnp.dot(pwb_ref[...], hi_ref[j], preferred_element_type=f32)
            second = jnp.dot(pwb_ref[:rows, :], lo_ref[j], preferred_element_type=f32)
            back.append(first[:rows] + first[rows:] + second)
        back = mixed(jnp.concatenate(back, axis=1))
        start = pl.multiple_of(m * 2 * rows, 2 * rows)
        back_ref[pl.ds(start, rows), :] = back[:, :atoms]
        back_ref[pl.ds(start + rows, rows), :] = back[:, atoms:]
        return carry

    lax.fori_loop(0, couples, body, 0)
    ham_ref[...] = jnp.dot(gyb_ref[...], back_ref[...], preferred_element_type=f32)
    sums = [
        jnp.sum(eacc_ref[j] * weight_ref[...], axis=0, keepdims=True) for j in range(chunks)
    ]
    sums = jnp.concatenate(sums, axis=1)
    energy_ref[...] = jnp.broadcast_to(
        -(sums[:, :atoms] + sums[:, atoms:]), energy_ref.shape
    )

def prepare(gaunt, pair_waves, y_table, core, radial_weights):
    entries = gaunt.shape[0]
    harmonics, directions = y_table.shape
    pairs, grid_points = pair_waves.shape
    rows = round_up(3 * pairs, 16)
    extra = rows - 3 * pairs
    assert directions % 2 == 0
    fused = jnp.einsum(
        "plq,ln->nqp", gaunt.reshape(entries, harmonics, pairs), y_table, precision=highest
    )

    hi, lo = split(fused)
    wide = lambda a, b, c: jnp.pad(
        jnp.concatenate([a, b, c], axis=1), ((0, 0), (0, extra), (0, 0))
    )
    hi3 = wide(hi, hi, hi)
    lo3 = wide(lo, lo, lo)
    gy = jnp.concatenate([hi3, hi3, lo3], axis=2).reshape(directions // 2, 2 * rows, 3 * entries)
    gyb = wide(hi, hi, lo).reshape(directions * rows, entries).T
    pw_hi, pw_lo = split(pair_waves)
    pw = jnp.pad(jnp.concatenate([pw_hi, pw_hi, pw_lo], axis=0), ((0, extra), (0, 0))).T
    point_weight = 4.0 * jnp.pi / directions * radial_weights
    b_hi, b_lo = split(-point_weight[None, :] * pair_waves)
    triple = lambda x: jnp.pad(jnp.concatenate([x, x, x], axis=0), ((0, extra), (0, 0)))
    pwb = jnp.concatenate([triple(b_hi), triple(b_lo)], axis=0)
    core_wide = jnp.broadcast_to(core[:, None], (grid_points, WIDE))
    weight_wide = jnp.broadcast_to(point_weight[:, None], (grid_points, WIDE))
    return gy, gyb, pw, pwb, core_wide, weight_wide

def local_energy(columns, tables, pairs):
    entries, atoms = columns.shape
    gy, gyb, pw, pwb, core_wide, weight_wide = tables
    grid_points, rows = pw.shape
    hi, lo = split(columns)
    dens = jnp.concatenate([hi, lo, hi], axis=0)
    chunks = 2 * atoms // WIDE
    step = 80 if grid_points % 80 == 0 else grid_points

    ham, energy = pl.pallas_call(
        lambda *refs: atom_kernel(*refs, pairs=pairs, step=step),
        out_shape=(
            jax.ShapeDtypeStruct((entries, atoms), f32),
            jax.ShapeDtypeStruct((8, atoms), f32),
        ),
        scratch_shapes=[
            pltpu.VMEM((chunks, grid_points, WIDE), f32),
            pltpu.VMEM((chunks, grid_points, WIDE), bf16),
            pltpu.VMEM((chunks, grid_points, WIDE), bf16),
            pltpu.VMEM((chunks, grid_points, WIDE), f32),
            pltpu.VMEM((gyb.shape[1], atoms), bf16),
        ],
        compiler_params=pltpu.CompilerParams(vmem_limit_bytes=48 * 1024 * 1024),
        name="atoms",
    )(dens, gy, gyb, pw, pwb, core_wide, weight_wide)
    return ham, energy[:1]

def per_device(dens_part, counts, gaunt, pair_waves, y_table, core, radial_weights):
    band_count = lax.axis_size("band")
    domain_count = lax.axis_size("domain")
    workers = band_count * domain_count
    axes = ("domain", "band")
    me = lax.axis_index("domain") * band_count + lax.axis_index("band")
    entries = dens_part.shape[1]
    slot_total = dens_part.shape[2]
    share = slot_total // band_count
    capacity = -(-share // workers)
    worker_rows = -(-(slot_total // 3) // band_count)
    atoms = round_up(worker_rows, LANES)
    tables = prepare(gaunt, pair_waves, y_table, core, radial_weights)

    own_cols = lax.psum_scatter(dens_part[0], "band", scatter_dimension=1, tiled=True)
    every_count = lax.all_gather(counts, "domain", axis=0, tiled=True)
    band_ids = jnp.arange(band_count, dtype=jnp.int32)
    live = jnp.clip(every_count[:, None] - band_ids[None, :] * share, 0, share).reshape(-1)
    ids = jnp.arange(workers, dtype=jnp.int32)
    starts = jnp.sum(jnp.where(ids[None, :] < ids[:, None], live[None, :], 0), axis=1)
    ends = starts + live
    own_start = jnp.sum(jnp.where(ids == me, starts, 0))
    own_live = jnp.sum(jnp.where(ids == me, live, 0))
    is_alive = jnp.arange(share, dtype=jnp.int32) < own_live

    own_cols = jnp.where(is_alive[None, :], own_cols, 0.0)
    own_cols = jnp.pad(own_cols, ((0, 0), (0, capacity * workers - share)))
    blocks = own_cols.T.reshape(capacity, workers, entries).transpose(1, 0, 2)
    outgoing = jnp.roll(blocks, own_start % workers, axis=0)
    incoming = lax.all_to_all(outgoing, axes, split_axis=0, concat_axis=0, tiled=True)

    atom_ids = jnp.arange(atoms, dtype=jnp.int32) * workers + me
    source = jnp.sum((ends[None, :] <= atom_ids[:, None]).astype(jnp.int32), axis=1)
    source = jnp.minimum(source, workers - 1)
    source_start = jnp.sum(jnp.where(source[:, None] == ids[None, :], starts[None, :], 0), axis=1)
    position = jnp.clip((atom_ids - source_start) // workers, 0, capacity - 1)
    compact = jnp.take(
        incoming.reshape(workers * capacity, entries), source * capacity + position, axis=0,
        mode="clip",
    )
    ham, energy = local_energy(compact.T, tables, pair_waves.shape[0])
    result = jnp.concatenate([ham, energy], axis=0).T
    row = (me - starts) % workers
    first = (starts + row - me) // workers
    target = first[:, None] + jnp.arange(capacity, dtype=jnp.int32)[None, :]
    back = jnp.take(result, jnp.clip(target, 0, atoms - 1).reshape(-1), axis=0, mode="clip")
    returned = lax.all_to_all(
        back.reshape(workers, capacity, entries + 1), axes, split_axis=0, concat_axis=0, tiled=True
    )
    returned = jnp.roll(returned, -(own_start % workers), axis=0)
    final = returned.transpose(1, 0, 2).reshape(capacity * workers, entries + 1).T[:, :share]
    final = jnp.where(is_alive[None, :], final, 0.0)
    whole = lax.all_gather(final, "band", axis=1, tiled=True)
    return whole[:entries], whole[entries]

def solution(mesh):
    return jax.shard_map(
        per_device,
        mesh=mesh,
        in_specs=(P("band", None, "domain"), P("domain"), P(), P(), P(), P(), P()),
        out_specs=(P(None, "domain"), P("domain")),
        check_vma=False,
    )
```

time: 542 us -> 227 us (0.42); the launches traced: 533 us -> 226 us
  matrix products: 334 us -> 1.18 us
  Pallas kernels: 0 us -> 43.2 us
  waiting for transfers between devices: 66.2 us -> 105 us
  local copies, waits for them, and re-layouts: 62.2 us -> 26.8 us
  blocking collectives: 31.8 us -> 13.8 us
    dot_general x8 -> x1, matrix products: 330 us -> 1.18 us  [prepare(): jnp.einsum('plq,ln->nqp', gaunt.reshape(entries, harmonics, pairs), y_tab...]
    pallas_call x0 -> x1, Pallas kernels: none -> 43.2 us  [local_energy(): pl.pallas_call(lambda *refs: atom_kernel(*refs, pairs=pairs, step=step),...]
    all_gather x1, waiting for transfers between devices: 0.01 us -> 35.2 us  [per_device(): whole = lax.all_gather(final, 'band', axis=1, tiled=True)]
    reshape x7 -> x4, local copies, waits for them, and re-layouts: 33.1 us -> 3.65 us  [the longest x1 1.42 us: per_device(): incoming.reshape(workers * capacity, entries)]
    all_to_all x2, waiting for transfers between devices: 47.3 us -> 62.7 us  [the longest x1 31.7 us: per_device(): lax.all_to_all(back.reshape(workers, capacity, entries + 1), axes, split_...]
    all_to_all x1 -> x0, blocking collectives: 13.7 us -> none  [per_device(): lax.all_to_all(back_energy.reshape(domain_count, capacity), 'domain', spl...]
    reduce_scatter x1, waiting for transfers between devices: 18.9 us -> 7 us  [per_device(): lax.psum_scatter(dens_part[0], 'band', scatter_dimension=1, tiled=True)]
    gather x3, local copies, waits for them, and re-layouts: 13.2 us -> 5.08 us  [the longest x1 3.27 us: per_device(): jnp.take(result, jnp.clip(target, 0, atoms - 1).reshape(-1), axis=0, mode...]
  transfers between devices with their start and end apart: 4 -> 4, of which waited for: 3 -> 4; matrix products, arithmetic and copies ran while one was open for 4% -> 6% of each run, Pallas kernels for 0% -> 0%
where the time goes in v1:
time: 227 us; the launch traced here: 226 us
  waiting for transfers between devices  105 us (46%)
  Pallas kernels  43.2 us (19%)
  local copies, waits for them, and re-layouts  26.8 us (12%)
  between operations  17.1 us (8%)
  blocking collectives  13.8 us (6%)
  other arithmetic  10.3 us (5%)
  starting transfers between devices  8.61 us (4%)
    pallas_call x1, Pallas kernels, local_energy(): pl.pallas_call(lambda *refs: atom_kernel(*refs, pairs=pairs, step=step),...  43.2 us
    all_gather x1, waiting for transfers between devices, per_device(): whole = lax.all_gather(final, 'band', axis=1, tiled=True)  35.2 us
    all_to_all x1, waiting for transfers between devices, per_device(): lax.all_to_all(back.reshape(workers, capacity, entries + 1), axes, split_...  31.7 us
    all_to_all x1, waiting for transfers between devices, per_device(): lax.all_to_all(outgoing, axes, split_axis=0, concat_axis=0, tiled=True)  30.9 us
    unnamed x1, blocking collectives  13.8 us
    unnamed x22, local copies, waits for them, and re-layouts  10.6 us
    reduce_scatter x1, waiting for transfers between devices, per_device(): lax.psum_scatter(dens_part[0], 'band', scatter_dimension=1, tiled=True)  7 us
    all_to_all x1, starting transfers between devices, per_device(): lax.all_to_all(outgoing, axes, split_axis=0, concat_axis=0, tiled=True)  4.9 us
  transfers between devices with their start and end apart: 4, of which 4 were waited for; matrix products, arithmetic and copies ran while one was open for 6% of the time, Pallas kernels for 0%

profile of v1, /device:TPU:0, one launch (start us, length us, event | category | flops | bytes accessed | tf_op | source)
XLA Modules:
  0.0 226.0 jit_solution(6929270312736835491)
XLA Ops:
  7.2 5.1 %copy.70 = f32[1,171,2304]{1,2,0:T(8,128)} copy(f32[1,171,2304]{2,0,1:T(1,128)} %param.7) | data formatting | bytes 3151872 | tf_op args[0]
  13.1 0.6 dynamic-slice
  13.6 0.8 dynamic-update-slice
  14.4 13.8 %all-reduce.6 = s32[16]{0:T(128)S(1)} all-reduce(s32[16]{0:T(128)S(1)} %dynamic-update-slice), channel_id=1, replica_groups=mesh['band'=2,'domain'=16] {'domain'}, use_global_device_ids=true, to_apply=%add.6 | all-reduce | flops 16 | bytes 128
  28.2 0.7 select_reduce_fusion.2
  29.1 0.6 and_select_fusion.1
  32.0 1.2 reduce-precision_convert_fusion
  33.2 0.9 pad_maximum_fusion
  34.4 3.1 %fusion.1 = bf16[50,64,513]{2,0,1:T(8,128)(2,1)S(1)} fusion(bf16[50,63,171]{2,0,1:T(8,128)(2,1)S(1)} %get-tuple-element.20, bf16[50,64,171]{2,0,1:T(8,128)(2,1)S(1)} %pad.20), kind=kLoop, calls=%fused_computation.4 | loop fusion | flops 13132800 | bytes 5454900 | tf_op jit(solution)/shard_map/concatenate | solution.py:101
  37.5 2.7 %copy.75 = bf16[50,64,513]{2,1,0:T(8,128)(2,1)} copy(bf16[50,64,513]{2,0,1:T(8,128)(2,1)S(1)} %fusion.1) | data formatting | bytes 6566400 | tf_op jit(solution)/shard_map/concatenate | solution.py:101
  40.2 0.4 copy.84
  40.6 0.4 pad.22.clone
  41.0 1.0 copy.77
  42.4 0.7 iota_compare_fusion.5
  43.0 7.0 %reduce-scatter.2.cloned.1.call-done = f32[171,1152]{0,1:T(8,128)} async-done(((f32[171,2304]{0,1:T(8,128)}), f32[171,1152]{0,1:T(8,128)}) %reduce-scatter.2.cloned.1.call-update) | async-done | bytes 787984 | tf_op jit(solution)/shard_map/reduce_scatter | solution.py:154
  50.0 1.5 broadcast_select_fusion
  51.9 1.7 copy.71
  53.6 4.9 %all-to-all-start = ((f32[32,36,171]{2,1,0:T(8,128)}), f32[32,36,171]{2,1,0:T(8,128)}, u32[]{:S(2)}, u32[]{:S(2)}) async-start(f32[32,36,171]{2,1,0:T(8,128)} %copy.71), calls=%async_computation.1 | async-start | bytes 2621440 | tf_op jit(solution)/shard_map/all_to_all | solution.py:169
  59.2 30.9 %all-to-all-done = f32[32,36,171]{2,1,0:T(8,128)} async-done(((f32[32,36,171]{2,1,0:T(8,128)}), f32[32,36,171]{2,1,0:T(8,128)}, u32[]{:S(2)}, u32[]{:S(2)}) %all-to-all-start) | async-done | bytes 788000 | tf_op jit(solution)/shard_map/all_to_all | solution.py:169
  90.2 1.4 reshape.219
  91.6 1.7 gather_fusion
  93.6 0.4 copy-done.4
  94.2 43.2 %atoms.1 = (f32[171,384]{1,0:T(8,128)S(1)}, f32[8,384]{1,0:T(8,128)S(1)}) custom-call(bf16[513,384]{1,0:T(8,128)(2,1)S(1)} %pad_maximum_fusion.4.refs_0_, bf16[25,128,513]{2,1,0:T(8,128)(2,1)} %bitcast.33, bf16[171,3200]{1,0:T(8,128)(2,1)S(1)} %bitcast.32, bf16[400,64]{1,0:T(8,128)(2,1)S(1)} %fusion.19.refs_3_, ...), custom_call_target="tpu_custom_call" | custom-call | tf_op jit(solution)/shard_map/atoms/pallas_call | solution.py:122
  137.7 3.3 %gather_fusion.1 = f32[1152,172]{1,0:T(8,128)S(1)} fusion(f32[384,172]{1,0:T(8,128)S(1)} %copy.81, s32[2048]{0:T(1024)S(1)} %pad_clamp_fusion), kind=kCustom, calls=%fused_computation.1 | custom fusion | bytes 1589760 | tf_op jit(solution)/shard_map/jit(_take)/gather | solution.py:185
  141.0 1.2 reshape.223
  142.1 3.6 %all-to-all-start.1 = ((f32[32,36,172]{2,1,0:T(8,128)}), f32[32,36,172]{2,1,0:T(8,128)S(1)}, u32[]{:S(2)}, u32[]{:S(2)}) async-start(f32[32,36,172]{2,1,0:T(8,128)} %reshape.223), calls=%async_computation.2 | async-start | bytes 2621440 | tf_op jit(solution)/shard_map/all_to_all | solution.py:186
  145.8 31.7 %all-to-all-done.1 = f32[32,36,172]{2,1,0:T(8,128)S(1)} async-done(((f32[32,36,172]{2,1,0:T(8,128)}), f32[32,36,172]{2,1,0:T(8,128)S(1)}, u32[]{:S(2)}, u32[]{:S(2)}) %all-to-all-start.1) | async-done | bytes 792608 | tf_op jit(solution)/shard_map/all_to_all | solution.py:186
  177.9 0.4 copy.82
  178.3 1.2 bitcast_select_fusion
  179.6 35.2 %all-gather.2.cloned.1.call-done = f32[172,2304]{0,1:T(8,128)} async-done(((f32[172,1152]{0,1:T(8,128)}), f32[172,2304]{0,1:T(8,128)}) %all-gather.2.cloned.1.call-update) | async-done | bytes 1585168 | tf_op jit(solution)/shard_map/all_gather | solution.py:192
  214.8 3.0 %copy.83 = f32[171,2304]{1,0:T(8,128)} copy(f32[171,2304]{0,1:T(8,128)} %bitcast.36) | data formatting | bytes 3151872
  217.8 1.3 slice_reduce_fusion
  (51 shorter events, 3.2 us)
Async XLA Ops:
  7.2 24.8 %copy-start = (f32[25,50]{1,0:T(8,128)S(1)}, f32[25,50]{1,0:T(8,128)}, u32[]{:S(2)}) copy-start(f32[25,50]{1,0:T(8,128)} %param.11) | copy-start | bytes 15004
  7.2 42.8 %reduce-scatter.2.cloned.1.call-start = ((), (), s32[]{:S(2)}) async-start(), calls=%async_computation.3 | async-start | bytes 3538944 | tf_op jit(solution)/shard_map/reduce_scatter | solution.py:154
  12.3 0.7 copy-start.6
  12.3 19.4 %copy-start.2 = (f32[171,525]{1,0:T(8,128)S(1)}, f32[171,525]{1,0:T(8,128)}, u32[]{:S(2)}) copy-start(f32[171,525]{1,0:T(8,128)} %param.9) | copy-start | bytes 1077304
  41.0 1.0 copy-start.3
  41.0 1.1 copy-start.5
  53.6 36.5 %all-to-all-start = ((f32[32,36,171]{2,1,0:T(8,128)}), f32[32,36,171]{2,1,0:T(8,128)}, u32[]{:S(2)}, u32[]{:S(2)}) async-start(f32[32,36,171]{2,1,0:T(8,128)} %copy.71), calls=%async_computation.1 | async-start | bytes 2621440 | tf_op jit(solution)/shard_map/all_to_all | solution.py:169
  93.3 0.7 copy-start.4
  142.1 35.5 %all-to-all-start.1 = ((f32[32,36,172]{2,1,0:T(8,128)}), f32[32,36,172]{2,1,0:T(8,128)S(1)}, u32[]{:S(2)}, u32[]{:S(2)}) async-start(f32[32,36,172]{2,1,0:T(8,128)} %reshape.223), calls=%async_computation.2 | async-start | bytes 2621440 | tf_op jit(solution)/shard_map/all_to_all | solution.py:186
  145.8 69.0 %all-gather.2.cloned.1.call-start = ((), (), s32[]{:S(2)}) async-start(), calls=%async_computation.4 | async-start | bytes 3538944 | tf_op jit(solution)/shard_map/all_gather | solution.py:192
  214.8 3.0 %copy-start.1 = (f32[172,2304]{0,1:T(8,128)S(1)}, f32[172,2304]{0,1:T(8,128)}, u32[]{:S(2)}) copy-start(f32[172,2304]{0,1:T(8,128)} %all-gather.2.cloned.1.call-done) | copy-start | bytes 4755460
Sparse Core Ops, SparseCore 0:
  12.5 37.5 reduce-scatter.1
  179.7 35.0 all-gather.1

commit v2 on v1

--- a/solution.py
+++ b/solution.py
@@ -187,9 +187,17 @@
         back.reshape(workers, capacity, entries + 1), axes, split_axis=0, concat_axis=0, tiled=True
     )
     returned = jnp.roll(returned, -(own_start % workers), axis=0)
-    final = returned.transpose(1, 0, 2).reshape(capacity * workers, entries + 1).T[:, :share]
-    final = jnp.where(is_alive[None, :], final, 0.0)
-    whole = lax.all_gather(final, "band", axis=1, tiled=True)
+    piece = returned.transpose(1, 0, 2).reshape(capacity * workers, entries + 1)[:share]
+    piece = jnp.where(is_alive[:, None], piece, 0.0)
+    band = lax.axis_index("band")
+    whole = jnp.zeros((slot_total, entries + 1), f32)
+    ring = [(i, (i + 1) % band_count) for i in range(band_count)]
+    for hop in range(band_count):
+        owner = (band - hop) % band_count
+        whole = lax.dynamic_update_slice(whole, piece, (owner * share, 0))
+        if hop + 1 < band_count:
+            piece = lax.ppermute(piece, "band", ring)
+    whole = whole.T
     return whole[:entries], whole[entries]
 
 def solution(mesh):

time: 227 us -> 207 us (0.912)
  waiting for transfers between devices: 105 us -> 87.6 us
  local copies, waits for them, and re-layouts: 26.8 us -> 24.1 us
    all_gather x1 -> x0, waiting for transfers between devices: 35.2 us -> none  [per_device(): whole = lax.all_gather(final, 'band', axis=1, tiled=True)]
    ppermute x0 -> x1, waiting for transfers between devices: none -> 17.9 us  [per_device(): piece = lax.ppermute(piece, 'band', ring)]
    unnamed x22 -> x21, local copies, waits for them, and re-layouts: 10.6 us -> 7.9 us
  transfers between devices with their start and end apart: 4 -> 4, of which waited for: 4 -> 4; matrix products, arithmetic and copies ran while one was open for 6% -> 7% of each run, Pallas kernels for 0% -> 0%
where the time goes in v2:
time: 207 us
  waiting for transfers between devices  87.6 us (42%)
  Pallas kernels  43.6 us (21%)
  local copies, waits for them, and re-layouts  24.1 us (12%)
  between operations  17.1 us (8%)
  blocking collectives  13.8 us (7%)
  starting transfers between devices  10.2 us (5%)
  other arithmetic  9.25 us (4%)
    pallas_call x1, Pallas kernels, local_energy(): pl.pallas_call(lambda *refs: atom_kernel(*refs, pairs=pairs, step=step),...  43.6 us
    all_to_all x1, waiting for transfers between devices, per_device(): lax.all_to_all(back.reshape(workers, capacity, entries + 1), axes, split_...  31.8 us
    all_to_all x1, waiting for transfers between devices, per_device(): lax.all_to_all(outgoing, axes, split_axis=0, concat_axis=0, tiled=True)  30.9 us
    ppermute x1, waiting for transfers between devices, per_device(): piece = lax.ppermute(piece, 'band', ring)  17.9 us
    unnamed x1, blocking collectives  13.8 us
    unnamed x21, local copies, waits for them, and re-layouts  7.9 us
    reduce_scatter x1, waiting for transfers between devices, per_device(): lax.psum_scatter(dens_part[0], 'band', scatter_dimension=1, tiled=True)  6.99 us
    all_to_all x1, starting transfers between devices, per_device(): lax.all_to_all(outgoing, axes, split_axis=0, concat_axis=0, tiled=True)  4.91 us
  transfers between devices with their start and end apart: 4, of which 4 were waited for; matrix products, arithmetic and copies ran while one was open for 7% of the time, Pallas kernels for 0%

profile of v2, /device:TPU:0, one launch (start us, length us, event | category | flops | bytes accessed | tf_op | source)
XLA Modules:
  0.0 206.9 jit_solution(14510031939647462586)
XLA Ops:
  7.2 5.1 %copy.60 = f32[1,171,2304]{1,2,0:T(8,128)} copy(f32[1,171,2304]{2,0,1:T(1,128)} %param.7) | data formatting | bytes 3151872 | tf_op args[0]
  13.1 0.6 dynamic-slice
  13.6 0.8 dynamic-update-slice
  14.4 13.8 %all-reduce.6 = s32[16]{0:T(128)S(1)} all-reduce(s32[16]{0:T(128)S(1)} %dynamic-update-slice), channel_id=1, replica_groups=mesh['band'=2,'domain'=16] {'domain'}, use_global_device_ids=true, to_apply=%add.6 | all-reduce | flops 16 | bytes 128
  28.2 0.7 select_reduce_fusion.2
  29.1 0.6 and_select_fusion.1
  32.0 1.2 reduce-precision_convert_fusion
  33.2 0.9 pad_maximum_fusion
  34.4 3.1 %fusion.1 = bf16[50,64,513]{2,0,1:T(8,128)(2,1)S(1)} fusion(bf16[50,63,171]{2,0,1:T(8,128)(2,1)S(1)} %get-tuple-element.10, bf16[50,64,171]{2,0,1:T(8,128)(2,1)S(1)} %pad.20), kind=kLoop, calls=%fused_computation.4 | loop fusion | flops 13132800 | bytes 5454900 | tf_op jit(solution)/shard_map/concatenate | solution.py:101
  37.6 2.7 %copy.65 = bf16[50,64,513]{2,1,0:T(8,128)(2,1)} copy(bf16[50,64,513]{2,0,1:T(8,128)(2,1)S(1)} %fusion.1) | data formatting | bytes 6566400 | tf_op jit(solution)/shard_map/concatenate | solution.py:101
  40.6 0.4 copy.75
  40.9 0.4 pad.22.clone
  41.4 1.0 copy.67
  42.4 0.7 iota_compare_fusion.5
  43.0 7.0 %reduce-scatter.2.cloned.1.call-done = f32[171,1152]{0,1:T(8,128)} async-done(((f32[171,2304]{0,1:T(8,128)}), f32[171,1152]{0,1:T(8,128)}) %reduce-scatter.2.cloned.1.call-update) | async-done | bytes 787984 | tf_op jit(solution)/shard_map/reduce_scatter | solution.py:154
  50.0 1.5 broadcast_select_fusion
  51.5 0.4 fusion.5
  51.9 1.7 copy.61
  53.6 4.9 %all-to-all-start = ((f32[32,36,171]{2,1,0:T(8,128)}), f32[32,36,171]{2,1,0:T(8,128)}, u32[]{:S(2)}, u32[]{:S(2)}) async-start(f32[32,36,171]{2,1,0:T(8,128)} %copy.61), calls=%async_computation.1 | async-start | bytes 2621440 | tf_op jit(solution)/shard_map/all_to_all | solution.py:169
  59.2 30.9 %all-to-all-done = f32[32,36,171]{2,1,0:T(8,128)} async-done(((f32[32,36,171]{2,1,0:T(8,128)}), f32[32,36,171]{2,1,0:T(8,128)}, u32[]{:S(2)}, u32[]{:S(2)}) %all-to-all-start) | async-done | bytes 788000 | tf_op jit(solution)/shard_map/all_to_all | solution.py:169
  90.2 1.4 reshape.223
  91.6 1.7 gather_fusion
  94.1 43.6 %atoms.1 = (f32[171,384]{1,0:T(8,128)S(1)}, f32[8,384]{1,0:T(8,128)S(1)}) custom-call(bf16[513,384]{1,0:T(8,128)(2,1)S(1)} %pad_maximum_fusion.4.refs_0_, bf16[25,128,513]{2,1,0:T(8,128)(2,1)} %bitcast.33, bf16[171,3200]{1,0:T(8,128)(2,1)S(1)} %bitcast.32, bf16[400,64]{1,0:T(8,128)(2,1)S(1)} %fusion.19.refs_3_, ...), custom_call_target="tpu_custom_call" | custom-call | tf_op jit(solution)/shard_map/atoms/pallas_call | solution.py:122
  138.0 3.3 %gather_fusion.1 = f32[1152,172]{1,0:T(8,128)S(1)} fusion(f32[384,172]{1,0:T(8,128)S(1)} %copy.71, s32[2048]{0:T(1024)S(1)} %pad_clamp_fusion), kind=kCustom, calls=%fused_computation.1 | custom fusion | bytes 1589760 | tf_op jit(solution)/shard_map/jit(_take)/gather | solution.py:185
  141.2 1.2 reshape.227
  142.4 3.6 %all-to-all-start.1 = ((f32[32,36,172]{2,1,0:T(8,128)}), f32[32,36,172]{2,1,0:T(8,128)S(1)}, u32[]{:S(2)}, u32[]{:S(2)}) async-start(f32[32,36,172]{2,1,0:T(8,128)} %reshape.227), calls=%async_computation.2 | async-start | bytes 2621440 | tf_op jit(solution)/shard_map/all_to_all | solution.py:186
  146.1 31.8 %all-to-all-done.1 = f32[32,36,172]{2,1,0:T(8,128)S(1)} async-done(((f32[32,36,172]{2,1,0:T(8,128)}), f32[32,36,172]{2,1,0:T(8,128)S(1)}, u32[]{:S(2)}, u32[]{:S(2)}) %all-to-all-start.1) | async-done | bytes 792608 | tf_op jit(solution)/shard_map/all_to_all | solution.py:186
  178.2 0.4 copy.72
  179.2 1.6 collective-permute-start
  180.9 17.9 %collective-permute-done = f32[1152,172]{0,1:T(8,128)S(1)} collective-permute-done((f32[1152,172]{0,1:T(8,128)S(1)}, f32[1152,172]{0,1:T(8,128)S(1)}, u32[]{:S(2)}, u32[]{:S(2)}) %collective-permute-start) | collective-permute-done | bytes 792608 | tf_op jit(solution)/shard_map/ppermute | solution.py:199
  198.9 0.7 slice_reduce_fusion
  199.6 0.5 copy-done.1
  (53 shorter events, 3.9 us)
Async XLA Ops:
  7.2 24.8 %copy-start = (f32[25,50]{1,0:T(8,128)S(1)}, f32[25,50]{1,0:T(8,128)}, u32[]{:S(2)}) copy-start(f32[25,50]{1,0:T(8,128)} %param.11) | copy-start | bytes 15004
  7.2 42.8 %reduce-scatter.2.cloned.1.call-start = ((), (), s32[]{:S(2)}) async-start(), calls=%async_computation.3 | async-start | bytes 3538944 | tf_op jit(solution)/shard_map/reduce_scatter | solution.py:154
  12.3 0.7 copy-start.6
  12.3 19.4 %copy-start.2 = (f32[171,525]{1,0:T(8,128)S(1)}, f32[171,525]{1,0:T(8,128)}, u32[]{:S(2)}) copy-start(f32[171,525]{1,0:T(8,128)} %param.9) | copy-start | bytes 1077304
  37.5 2.7 %copy-start.3 = (f32[21,400]{1,0:T(8,128)S(1)}, f32[21,400]{1,0:T(8,128)}, u32[]{:S(2)}) copy-start(f32[21,400]{1,0:T(8,128)} %param.10) | copy-start | bytes 100804
  37.6 2.8 %copy-start.5 = (f32[400]{0:T(512)S(1)}, f32[400]{0:T(512)}, u32[]{:S(2)}) copy-start(f32[400]{0:T(512)} %param.13) | copy-start | bytes 4804
  53.6 36.6 %all-to-all-start = ((f32[32,36,171]{2,1,0:T(8,128)}), f32[32,36,171]{2,1,0:T(8,128)}, u32[]{:S(2)}, u32[]{:S(2)}) async-start(f32[32,36,171]{2,1,0:T(8,128)} %copy.61), calls=%async_computation.1 | async-start | bytes 2621440 | tf_op jit(solution)/shard_map/all_to_all | solution.py:169
  93.3 0.7 copy-start.4
  142.4 35.4 %all-to-all-start.1 = ((f32[32,36,172]{2,1,0:T(8,128)}), f32[32,36,172]{2,1,0:T(8,128)S(1)}, u32[]{:S(2)}, u32[]{:S(2)}) async-start(f32[32,36,172]{2,1,0:T(8,128)} %reshape.227), calls=%async_computation.2 | async-start | bytes 2621440 | tf_op jit(solution)/shard_map/all_to_all | solution.py:186
  179.2 19.6 %collective-permute-start = (f32[1152,172]{0,1:T(8,128)S(1)}, f32[1152,172]{0,1:T(8,128)S(1)}, u32[]{:S(2)}, u32[]{:S(2)}) collective-permute-start(f32[1152,172]{0,1:T(8,128)S(1)} %copy.73), channel_id=1, source_target_pairs={{0,16},{16,0},{1,17},{17,1},{2,18},{18,2},{3,19},{19,3},{4,20},{20... | collective-permute-start | bytes 2377736 | tf_op jit(solution)/shard_map/ppermute | solution.py:199
  198.9 1.2 copy-start.1
Sparse Core Ops, SparseCore 0:
  12.5 37.5 reduce-scatter.1
